TPU v7x, 32 devices: a whole 2x2x4 slice. The times are simulated.
32 devices in a mesh: ha: 8 (over z, core), wa: 2 (over y), ba: 2 (over x).
Axes of the slice: x: 2, y: 2, z: 4, core: 2. Of those that a mesh axis runs over, the one named last changes fastest.
Arguments:
- tokens: bfloat16 [2, 128, 64, 384], P('ba', 'ha', 'wa'), may hold values from -6 to 6
- cotangent: bfloat16 [2, 128, 64, 384], P('ba', 'ha', 'wa'), may hold values from -6 to 6
- w_qkv: bfloat16 [384, 1152], replicated, may hold values from -0.20412415 to 0.20412415
- w_proj: bfloat16 [384, 384], replicated, may hold values from -0.3125 to 0.3125
- table_logits: float32 [12, 225], replicated, may hold values from -6 to 6
- logit_scale: float32 [12], replicated, may hold values from 1 to 5.5
- gain: float32 [384], replicated, may hold values from 0.5 to 1.5
Outputs:
- d_tokens: bfloat16 [2, 128, 64, 384], P('ba', 'ha', 'wa')
- d_wqkv: float32 [384, 1152], P(None, 'ba')
- d_wproj: float32 [384, 384], P(None, 'ba')
- d_table: float32 [12, 225], replicated
- d_scale: float32 [12], replicated
- d_gain: float32 [384], replicated
All inputs are finite; a program needn't handle non-finite values.
Results may differ from a plain program's by a relative error of at most 0.01.
The roundings to bfloat16 on the way count: a program that leaves them out, or rounds other values in their place, can miss the bound.
Values may be sent and summed in bfloat16 or wider, within the bound.
A program may use at most 64 MiB of HBM per device.

v0:
```python
import math
import jax
import jax.numpy as jnp
from jax import lax
from jax.sharding import PartitionSpec as P

WIN = 8
EPS_NORM = 1e-05
MASK_FILL = -100.0
SCALE_CAP = math.log(100.0)
BIAS_RANGE = 16.0
HIGHEST = lax.Precision.HIGHEST


def from_behind(block, axis, distance):
    devices = range(lax.axis_size(axis))
    route = [((i - distance) % len(devices), i) for i in devices]
    return lax.ppermute(block, axis, route)


def coarse_product(form, left, right):
    return jnp.einsum(form, left, right, preferred_element_type=jnp.float32)


def fine_product(form, left, right):
    return jnp.einsum(form, left, right, precision=HIGHEST)


def to_windows(block, window):
    images, height, width, depth = block.shape
    tiles = block.reshape(images, height // window, window, width // window, window, depth)
    tiles = tiles.transpose(0, 1, 3, 2, 4, 5)
    return tiles.reshape(images, height // window * (width // window), window * window, depth)


def from_windows(tiles, images, height, width, window):
    depth = tiles.shape[-1]
    grid = tiles.reshape(images, height // window, width // window, window, window, depth)
    return grid.transpose(0, 1, 3, 2, 4, 5).reshape(images, height, width, depth)


def position_onehot(window):
    places = jnp.arange(window * window, dtype=jnp.int32)
    row_of = places // window
    col_of = places % window
    offset = (row_of[:, None] - row_of[None, :] + window - 1) * (2 * window - 1) + (
        col_of[:, None] - col_of[None, :] + window - 1
    )
    entries = jnp.arange((2 * window - 1) ** 2, dtype=jnp.int32)
    return (offset.reshape(-1)[:, None] == entries[None, :]).astype(jnp.float32)


def region_of(coords, extent, window):
    return (coords >= extent - window).astype(jnp.int32) + (coords >= extent - window // 2).astype(
        jnp.int32
    )


def region_mask(row_start, col_start, rows, cols, height, width, window):
    row_label = region_of(row_start + jnp.arange(rows, dtype=jnp.int32), height, window)
    col_label = region_of(col_start + jnp.arange(cols, dtype=jnp.int32), width, window)
    labels = row_label[:, None] * 3 + col_label[None, :]
    labels = labels.reshape(rows // window, window, cols // window, window).transpose(0, 2, 1, 3)
    labels = labels.reshape(-1, window * window)
    return jnp.where(labels[:, :, None] != labels[:, None, :], MASK_FILL, 0.0).astype(jnp.float32)


def grads_region(block, grad_block, row_start, col_start, height, width, window, params):
    w_qkv, w_proj, table_logits, logit_scale, gain = params
    images, rows, cols, depth = block.shape
    heads = logit_scale.shape[0]
    head_dim = depth // heads
    tiles = to_windows(block, window)
    grad_tiles = to_windows(grad_block, window)
    count = tiles.shape[1]
    length = window * window
    flat = tiles.reshape(-1, depth)
    qkv = jnp.dot(flat, w_qkv, preferred_element_type=jnp.float32).astype(jnp.bfloat16)
    qkv = qkv.reshape(images, count, length, 3, heads, head_dim)
    query = qkv[:, :, :, 0].astype(jnp.float32)
    keys = qkv[:, :, :, 1].astype(jnp.float32)
    values = qkv[:, :, :, 2]
    query_inv = lax.rsqrt(jnp.sum(query * query, -1, keepdims=True) + 1.0)
    key_inv = lax.rsqrt(jnp.sum(keys * keys, -1, keepdims=True) + 1.0)
    unit_query = query * query_inv
    unit_key = keys * key_inv
    scale = jnp.exp(jnp.minimum(logit_scale, SCALE_CAP))
    onehot = position_onehot(window)
    sigma = jax.nn.sigmoid(table_logits)
    rel_bias = jnp.dot(sigma * BIAS_RANGE, onehot.T, precision=HIGHEST).reshape(
        heads, length, length
    )
    mask = region_mask(row_start, col_start, rows, cols, height, width, window)
    cosine = fine_product("bnqhd,bnkhd->bnhqk", unit_query, unit_key)
    scores = scale[:, None, None] * cosine + rel_bias[None, None] + mask[None, :, None]
    top = jnp.max(scores, -1, keepdims=True)
    expo = jnp.exp(scores - top)
    probs = expo / jnp.sum(expo, -1, keepdims=True)
    probs_low = probs.astype(jnp.bfloat16)
    attended = (
        coarse_product("bnhqk,bnkhd->bnqhd", probs_low, values)
        .astype(jnp.bfloat16)
        .reshape(-1, depth)
    )
    proj = jnp.dot(attended, w_proj, preferred_element_type=jnp.float32)
    centre = proj - jnp.mean(proj, -1, keepdims=True)
    inv_std = lax.rsqrt(jnp.mean(centre * centre, -1, keepdims=True) + EPS_NORM)
    normed = centre * inv_std
    upstream = grad_tiles.reshape(-1, depth).astype(jnp.float32)
    d_gain = jnp.sum(upstream * normed, 0)
    scaled = upstream * gain
    d_proj = inv_std * (
        scaled
        - jnp.mean(scaled, -1, keepdims=True)
        - normed * jnp.mean(scaled * normed, -1, keepdims=True)
    )
    d_proj = d_proj.astype(jnp.bfloat16)
    d_wproj = jnp.dot(attended.T, d_proj, preferred_element_type=jnp.float32)
    d_att = jnp.dot(d_proj, w_proj.T, preferred_element_type=jnp.float32).astype(jnp.bfloat16)
    d_att = d_att.reshape(images, count, length, heads, head_dim)
    d_probs = coarse_product("bnqhd,bnkhd->bnhqk", d_att, values)
    d_values = coarse_product("bnhqk,bnqhd->bnkhd", probs_low, d_att)
    d_scores = probs * (d_probs - jnp.sum(d_probs * probs, -1, keepdims=True))
    d_bias = jnp.sum(d_scores, (0, 1)).reshape(heads, length * length)
    d_table = jnp.dot(d_bias, onehot, precision=HIGHEST) * (BIAS_RANGE * sigma * (1.0 - sigma))
    live = (logit_scale < SCALE_CAP).astype(jnp.float32)
    d_scale = jnp.sum(d_scores * cosine, (0, 1, 3, 4)) * scale * live
    d_cos = d_scores * scale[:, None, None]
    d_unit_q = fine_product("bnhqk,bnkhd->bnqhd", d_cos, unit_key)
    d_unit_k = fine_product("bnhqk,bnqhd->bnkhd", d_cos, unit_query)
    d_query = query_inv * (
        d_unit_q - unit_query * jnp.sum(unit_query * d_unit_q, -1, keepdims=True)
    )
    d_key = key_inv * (d_unit_k - unit_key * jnp.sum(unit_key * d_unit_k, -1, keepdims=True))
    d_qkv = jnp.stack([d_query, d_key, d_values], 3).astype(jnp.bfloat16).reshape(-1, 3 * depth)
    d_wqkv = jnp.dot(flat.T, d_qkv, preferred_element_type=jnp.float32)
    d_flat = jnp.dot(d_qkv, w_qkv.T, preferred_element_type=jnp.float32).astype(jnp.bfloat16)
    d_block = from_windows(d_flat.reshape(images, count, length, depth), images, rows, cols, window)
    return (d_block, (d_wqkv, d_wproj, d_table, d_scale, d_gain))


def shift_in(tokens, cotangent, shift):
    stacked = jnp.stack([tokens, cotangent])
    below = from_behind(stacked[:, :, :shift], "ha", -1)
    tall = jnp.concatenate([stacked[:, :, shift:], below], 2)
    beside = from_behind(tall[:, :, :, :shift], "wa", -1)
    moved = jnp.concatenate([tall[:, :, :, shift:], beside], 3)
    return (moved[0], moved[1])


def shift_out(grads, shift):
    rows = grads.shape[1]
    cols = grads.shape[2]
    right = from_behind(grads[:, :, cols - shift :], "wa", 1)
    wide = jnp.concatenate([right, grads[:, :, : cols - shift]], 2)
    lower = from_behind(wide[:, rows - shift :], "ha", 1)
    return jnp.concatenate([lower, wide[:, : rows - shift]], 1)


def shards(tokens, cotangent, w_qkv, w_proj, table_logits, logit_scale, gain):
    rows = tokens.shape[1]
    cols = tokens.shape[2]
    shift = WIN // 2
    height = rows * lax.axis_size("ha")
    width = cols * lax.axis_size("wa")
    row_base = lax.axis_index("ha") * rows
    col_base = lax.axis_index("wa") * cols
    params = (w_qkv, w_proj, table_logits, logit_scale, gain)
    moved, moved_grad = shift_in(tokens, cotangent, shift)
    d_moved, parts = grads_region(moved, moved_grad, row_base, col_base, height, width, WIN, params)
    back = shift_out(d_moved, shift)
    d_tokens = (cotangent.astype(jnp.float32) + back.astype(jnp.float32)).astype(jnp.bfloat16)
    d_wqkv, d_wproj, d_table, d_scale, d_gain = parts
    half_qkv, half_proj = (
        lax.psum_scatter(d_wqkv.astype(jnp.bfloat16), "ba", scatter_dimension=1, tiled=True).astype(
            jnp.float32
        ),
        lax.psum_scatter(
            d_wproj.astype(jnp.bfloat16), "ba", scatter_dimension=1, tiled=True
        ).astype(jnp.float32),
    )
    half_qkv, half_proj = lax.psum((half_qkv, half_proj), ("ha", "wa"))
    d_table, d_scale, d_gain = lax.psum((d_table, d_scale, d_gain), ("ha", "wa", "ba"))
    return (d_tokens, half_qkv, half_proj, d_table, d_scale, d_gain)


def solution(mesh):
    return jax.shard_map(
        shards,
        mesh=mesh,
        in_specs=(P("ba", "ha", "wa", None), P("ba", "ha", "wa", None), P(), P(), P(), P(), P()),
        out_specs=(P("ba", "ha", "wa", None), P(None, "ba"), P(None, "ba"), P(), P(), P()),
        check_vma=False,
    )
```

profile of v0, /device:TPU:0, one launch (start us, length us, event | category | flops | bytes accessed | tf_op | source)
XLA Modules:
  0.0 213.7 jit_solution(15621993046436900654)
XLA Ops:
  7.2 1.0 pad_maximum_fusion.2
  8.3 4.6 %collective-permute-start = (bf16[2,1,4,32,384]{4,3,2,1,0:T(8,128)(2,1)S(1)}, bf16[2,1,4,32,384]{4,3,2,1,0:T(8,128)(2,1)S(1)}, u32[]{:S(2)}, u32[]{:S(2)}) collective-permute-start(bf16[2,1,4,32,384]{4,3,2,1,0:T(8,128)(2,1)S(1)} %pad_maximum_fusion.2), channel_id=1, source_target_pairs={{4,0},{8,4},{12,8},{16,12},{20,16},{24,20},{28,24},{0,28},{5,1},{9... | collective-permute-start | bytes 589832 | tf_op jit(solution)/shard_map/ppermute | solution.py:18
  12.8 1.1 fusion.52
  14.2 0.8 compare_select_fusion
  15.2 2.0 fusion.2
  17.4 0.9 copy.85
  18.3 1.6 collective-permute-start.1
  20.2 2.8 %collective-permute-done.1 = bf16[2,1,16,4,384]{4,3,2,1,0:T(4,128)(2,1)S(1)} collective-permute-done((bf16[2,1,16,4,384]{4,3,2,1,0:T(4,128)(2,1)S(1)}, bf16[2,1,16,4,384]{4,3,2,1,0:T(4,128)(2,1)S(1)}, u32[]{:S(2)}, u32[]{:S(2)}) %collective-permute-start.1) | collective-permute-done | bytes 98336 | tf_op jit(solution)/shard_map/ppermute | solution.py:18
  23.0 0.9 fusion.57
  24.0 0.7 copy-done.9
  24.7 0.8 convolution_convert_fusion
  25.5 0.6 copy.82
  26.1 3.0 %reshape.449 = bf16[1,8,64,3,12,32]{2,1,5,4,3,0:T(8,128)(2,1)} reshape(bf16[512,1152]{0,1:T(8,128)(2,1)S(1)} %copy.82) | data formatting | bytes 2359296 | tf_op jit(solution)/shard_map/reshape | solution.py:79
  29.2 1.8 fusion.67
  31.7 5.2 %fusion.29 = f32[8,12,64,64]{2,3,1,0:T(8,128)S(1)} fusion(f32[8,64,12]{1,2,0:T(8,128)S(1)} %add_rsqrt_fusion.1, f32[8,64,12]{1,2,0:T(8,128)S(1)} %add_rsqrt_fusion, bf16[1,8,64,1,12,32]{2,1,5,4,3,0:T(8,128)(2,1)S(1)} %get-tuple-element.16, bf16[1,8,64,1,12,32]{2,1,5,4,3,0:T(8,128)(2,1)S(1)} %get-tuple-element.17), kind=kOutput, calls=%fused_computation.41 | convolution fusion | flops 151781376 | bytes 2408448 | tf_op jit(solution)/shard_map/bnqhd,bnkhd->bnhqk/dot_general | solution.py:26
  36.9 1.2 fusion.68
  38.2 0.5 copy-done.1
  38.6 0.5 fusion.40
  39.2 1.1 copy-done.3
  40.3 0.5 copy.88
  40.8 1.3 reshape.451
  42.1 1.6 fusion.69
  43.9 0.9 copy.89
  44.8 2.3 %copy.90 = f32[512,384]{0,1:T(8,128)} copy(f32[512,384]{1,0:T(8,128)} %bitcast.140) | data formatting | bytes 1572864 | tf_op jit(solution)/shard_map/convert_element_type | solution.py:109
  47.1 1.2 fusion.42
  48.3 1.4 multiply_reduce_fusion.2
  49.8 1.4 multiply_convert_fusion
  51.7 1.1 convolution_convert_fusion.5
  53.0 1.3 reshape.452
  54.3 3.6 %multiply_reduce_fusion.1 = (f32[8,12,64]{2,1,0:T(8,128)S(1)}, f32[8,12,64,64]{2,3,1,0:T(8,128)S(1)}) fusion(f32[8,12,64,64]{2,3,1,0:T(8,128)} %copy-done.3, f32[8,12,64]{2,1,0:T(8,128)S(1)} %get-tuple-element.21, bf16[1,8,64,1,12,32]{2,1,5,4,3,0:T(8,128)(2,1)} %copy-done.14, bf16[8,64,12,32]{1,0,3,2:T(8,128)(2,1)} %reshape.452), kind=kOutput, calls=%fused_computation.7 | convolution fusion | flops 26339328 | bytes 3981312 | tf_op jit(solution)/shard_map/bnqhd,bnkhd->bnhqk/dot_general | solution.py:22
  57.9 0.6 copy-done.4
  58.6 2.2 %multiply_reduce_fusion = (f32[12]{0:T(128)S(1)}, f32[12,64,64]{1,2,0:T(8,128)}, f32[8,12,64,64]{2,3,1,0:T(8,128)S(1)}) fusion(f32[8,12,64,64]{2,3,1,0:T(8,128)S(1)} %copy-done.2, f32[8,12,64,64]{2,3,1,0:T(8,128)S(1)} %get-tuple-element.26, f32[8,12,64]{2,1,0:T(8,128)S(1)} %get-tuple-element.25, f32[8,12,64,64]{2,3,1,0:T(8,128)S(1)} %copy-done.4, ...), kind=kLoop, calls=%fused_computation.5 | loop fusion | flops 2310132 | bytes 6537264 | tf_op jit(solution)/shard_map/reduce_sum | solution.py:127
  60.7 4.3 %fusion.22 = (f32[8,64,12]{1,2,0:T(8,128)S(1)}, f32[8,12,32,64]{3,2,1,0:T(8,128)}) fusion(f32[8,64,12]{1,2,0:T(8,128)S(1)} %add_rsqrt_fusion.1, bf16[1,8,64,1,12,32]{2,1,5,4,3,0:T(8,128)(2,1)S(1)} %get-tuple-element.17, f32[8,12,64,64]{2,3,1,0:T(8,128)S(1)} %get-tuple-element.15, f32[12]{0:T(128)S(1)} %minimum_exponential_fusion, ...), kind=kOutput, calls=%fused_computation.35 | convolution fusion | flops 152561664 | bytes 3219504 | tf_op jit(solution)/shard_map/bnhqk,bnkhd->bnqhd/dot_general | solution.py:26
  65.0 6.8 %fusion.18 = (f32[8,64,12]{1,2,0:T(8,128)}, f32[8,12,32,64]{3,2,1,0:T(8,128)}) fusion(f32[8,64,12]{1,2,0:T(8,128)S(1)} %add_rsqrt_fusion, bf16[1,8,64,1,12,32]{2,1,5,4,3,0:T(8,128)(2,1)S(1)} %get-tuple-element.16, f32[8,12,64,64]{2,3,1,0:T(8,128)S(1)} %get-tuple-element.15, f32[12]{0:T(128)S(1)} %minimum_exponential_fusion, ...), kind=kOutput, calls=%fused_computation.31 | convolution fusion | flops 152561664 | bytes 3219504 | tf_op jit(solution)/shard_map/bnhqk,bnqhd->bnkhd/dot_general | solution.py:26
  71.9 0.9 convolution_bitcast_fusion
  73.1 2.6 %fusion.21 = (bf16[1,8,64,1,12,32]{2,5,4,1,3,0:T(8,128)(2,1)S(1)}, bf16[1,8,64,1,12,32]{2,5,4,1,3,0:T(8,128)(2,1)S(1)}) fusion(f32[8,12,32,64]{3,2,1,0:T(8,128)} %get-tuple-element.28, f32[8,64,12]{1,2,0:T(8,128)} %get-tuple-element.27, f32[8,64,12]{1,2,0:T(8,128)S(1)} %add_rsqrt_fusion, bf16[1,8,64,1,12,32]{2,1,5,4,3,0:T(8,128)(2,1)S(1)} %get-tuple-element.16, ...), kind=kLoop, calls=%fused_computation.34 | loop fusion | flops 2359296 | bytes 3244032 | tf_op jit(solution)/shard_map/stack | solution.py:135
  75.7 0.6 maximum_convert_fusion
  76.3 2.7 %copy.98 = bf16[1,8,64,3,12,32]{2,1,5,4,3,0:T(8,128)(2,1)S(1)} copy(bf16[1,8,64,3,12,32]{2,5,4,1,3,0:T(8,128)(2,1)S(1)} %maximum_convert_fusion) | data formatting | bytes 2359296 | tf_op jit(solution)/shard_map/convert_element_type | solution.py:135
  79.1 2.4 %convert_element_type.207 = bf16[512,1152]{0,1:T(8,128)(2,1)} reshape(bf16[1,8,64,3,12,32]{2,1,5,4,3,0:T(8,128)(2,1)S(1)} %copy.98) | data formatting | bytes 2359296 | tf_op jit(solution)/shard_map/convert_element_type | solution.py:135
  81.5 3.1 %convolution_convert_fusion.1 = bf16[384,1152]{0,1:T(8,128)(2,1)} fusion(bf16[512,1152]{0,1:T(8,128)(2,1)} %convert_element_type.207, bf16[512,384]{1,0:T(8,128)(2,1)} %bitcast.142), kind=kOutput, calls=%fused_computation.15 | convolution fusion | flops 453427200 | bytes 2457600 | tf_op jit(solution)/shard_map/dot_general | solution.py:136
  84.9 0.9 copy-done.11
  85.8 0.9 convolution_convert_fusion.3
  86.8 1.6 collective-permute-start.2
  88.4 1.4 fusion.41
  89.8 1.1 collective-permute-done.2
  91.1 39.5 %all-reduce = (f32[12,225]{1,0:T(8,128)}, f32[12]{0:T(128)}, f32[384]{0:T(512)}) all-reduce(f32[12,225]{1,0:T(8,128)S(1)} %fusion.41, f32[12]{0:T(128)S(1)} %compare_select_fusion.1, f32[384]{0:T(512)S(1)} %get-tuple-element.8), channel_id=1, replica_groups=mesh['ha'=8,'wa'=2,'ba'=2] {'ha','wa','ba'}, use_global_device_ids=true, to_apply=%region_16.17 | all-reduce | flops 3096 | bytes 24768 | tf_op jit(solution)/shard_map/psum | solution.py:183
  130.6 0.9 add_convert_fusion
  131.5 75.2 %all-reduce.3 = (f32[384,576]{0,1:T(8,128)}, f32[384,192]{0,1:T(8,128)}) all-reduce(bf16[384,576]{0,1:T(8,128)(2,1)} %reduce-scatter.3.cloned.1.call-done, bf16[384,192]{0,1:T(8,128)(2,1)} %reduce-scatter.5.cloned.1.call-done), channel_id=1, replica_groups=mesh['ha'=8,'wa'=2,'ba'=2] {'ha','wa'}, use_global_device_ids=true, to_apply=%region_12.13 | all-reduce | flops 294912 | bytes 1769472 | tf_op jit(solution)/shard_map/psum | solution.py:182
  (75 shorter events, 3.4 us)
Async XLA Ops:
  7.2 17.5 %copy-start = (bf16[384,1152]{1,0:T(8,128)(2,1)S(1)}, bf16[384,1152]{1,0:T(8,128)(2,1)}, u32[]{:S(2)}) copy-start(bf16[384,1152]{1,0:T(8,128)(2,1)} %param.9) | copy-start | bytes 2654212
  7.2 8.0 %copy-start.17 = (f32[12,225]{1,0:T(8,128)S(1)}, f32[12,225]{1,0:T(8,128)}, u32[]{:S(2)}) copy-start(f32[12,225]{1,0:T(8,128)} %param.11) | copy-start | bytes 32404
  7.2 124.3 %reduce-scatter.5.cloned.1.call-start = ((), (), s32[]{:S(2)}) async-start(), calls=%async_computation.3 | async-start | bytes 442368 | tf_op jit(solution)/shard_map/reduce_scatter | solution.py:178
  8.3 10.0 %collective-permute-start = (bf16[2,1,4,32,384]{4,3,2,1,0:T(8,128)(2,1)S(1)}, bf16[2,1,4,32,384]{4,3,2,1,0:T(8,128)(2,1)S(1)}, u32[]{:S(2)}, u32[]{:S(2)}) collective-permute-start(bf16[2,1,4,32,384]{4,3,2,1,0:T(8,128)(2,1)S(1)} %pad_maximum_fusion.2), channel_id=1, source_target_pairs={{4,0},{8,4},{12,8},{16,12},{20,16},{24,20},{28,24},{0,28},{5,1},{9... | collective-permute-start | bytes 589832 | tf_op jit(solution)/shard_map/ppermute | solution.py:18
  14.0 4.3 %copy-start.18 = (f32[12]{0:T(128)S(1)}, f32[12]{0:T(128)}, u32[]{:S(2)}) copy-start(f32[12]{0:T(128)} %param.12) | copy-start | bytes 148
  18.3 4.7 %collective-permute-start.1 = (bf16[2,1,16,4,384]{4,3,2,1,0:T(4,128)(2,1)S(1)}, bf16[2,1,16,4,384]{4,3,2,1,0:T(4,128)(2,1)S(1)}, u32[]{:S(2)}, u32[]{:S(2)}) collective-permute-start(bf16[2,1,16,4,384]{4,3,2,1,0:T(4,128)(2,1)S(1)} %pad_maximum_fusion.4), channel_id=1, source_target_pairs={{2,0},{0,2},{3,1},{1,3},{6,4},{4,6},{7,5},{5,7},{10,8},{8,10},{11,... | collective-permute-start | bytes 294920 | tf_op jit(solution)/shard_map/ppermute | solution.py:18
  24.0 0.7 copy-start.9
  30.9 7.7 %copy-start.14 = (bf16[1,8,64,1,12,32]{2,1,5,4,3,0:T(8,128)(2,1)}, bf16[1,8,64,1,12,32]{2,1,5,4,3,0:T(8,128)(2,1)S(1)}, u32[]{:S(2)}) copy-start(bf16[1,8,64,1,12,32]{2,1,5,4,3,0:T(8,128)(2,1)S(1)} %get-tuple-element.18) | copy-start | bytes 1179652
  31.7 5.2 %copy-start.10 = (f32[12,64,64]{1,2,0:T(8,128)S(1)}, f32[12,64,64]{1,2,0:T(8,128)}, u32[]{:S(2)}) copy-start(f32[12,64,64]{1,2,0:T(8,128)} %copy.85) | copy-start | bytes 589828
  31.7 5.2 %copy-start.13 = (f32[8,64,64]{1,2,0:T(8,128)S(1)}, f32[8,64,64]{1,2,0:T(8,128)}, u32[]{:S(2)}) copy-start(f32[8,64,64]{1,2,0:T(8,128)} %compare_select_fusion) | copy-start | bytes 393220
  36.9 1.7 copy-start.1
  38.6 1.7 copy-start.3
  42.1 1.7 copy-start.6
  43.9 3.2 %copy-start.16 = (f32[384]{0:T(512)S(1)}, f32[384]{0:T(512)}, u32[]{:S(2)}) copy-start(f32[384]{0:T(512)} %param.13) | copy-start | bytes 4612
  49.8 1.4 copy-start.12
  49.8 1.9 copy-start.5
  54.3 3.6 %copy-start.2 = (f32[8,12,64,64]{2,3,1,0:T(8,128)S(1)}, f32[8,12,64,64]{2,3,1,0:T(8,128)}, u32[]{:S(2)}) copy-start(f32[8,12,64,64]{2,3,1,0:T(8,128)} %copy-done.1) | copy-start | bytes 4718596
  54.3 4.3 %copy-start.4 = (f32[8,12,64,64]{2,3,1,0:T(8,128)S(1)}, f32[8,12,64,64]{2,3,1,0:T(8,128)}, u32[]{:S(2)}) copy-start(f32[8,12,64,64]{2,3,1,0:T(8,128)} %copy-done.3) | copy-start | bytes 4718596
  65.0 6.8 %copy-start.15 = (bf16[8,64,12,32]{1,0,3,2:T(8,128)(2,1)S(1)}, bf16[8,64,12,32]{1,0,3,2:T(8,128)(2,1)}, u32[]{:S(2)}) copy-start(bf16[8,64,12,32]{1,0,3,2:T(8,128)(2,1)} %reshape.452) | copy-start | bytes 1179652
  72.8 58.7 %reduce-scatter.3.cloned.1.call-start = ((), (), s32[]{:S(2)}) async-start(), calls=%async_computation.2 | async-start | bytes 1327104 | tf_op jit(solution)/shard_map/reduce_scatter | solution.py:175
  81.5 3.1 %copy-start.8 = (f32[12,64,64]{1,2,0:T(8,128)S(1)}, f32[12,64,64]{1,2,0:T(8,128)}, u32[]{:S(2)}) copy-start(f32[12,64,64]{1,2,0:T(8,128)} %get-tuple-element.7) | copy-start | bytes 589828
  84.6 1.3 copy-start.11
  86.7 43.9 %copy-start.7 = (bf16[1,16,32,384]{3,2,1,0:T(8,128)(2,1)S(1)}, bf16[1,16,32,384]{3,2,1,0:T(8,128)(2,1)}, u32[]{:S(2)}) copy-start(bf16[1,16,32,384]{3,2,1,0:T(8,128)(2,1)} %param.8) | copy-start | bytes 1179652
  86.8 4.2 %collective-permute-start.2 = (bf16[1,16,4,384]{3,2,1,0:T(4,128)(2,1)S(1)}, bf16[1,16,4,384]{3,2,1,0:T(4,128)(2,1)S(1)}, u32[]{:S(2)}, u32[]{:S(2)}) collective-permute-start(bf16[1,16,4,384]{3,2,1,0:T(4,128)(2,1)S(1)} %slice.61), channel_id=1, source_target_pairs={{2,0},{0,2},{3,1},{1,3},{6,4},{4,6},{7,5},{5,7},{10,8},{8,10},{11,... | collective-permute-start | bytes 147464 | tf_op jit(solution)/shard_map/ppermute | solution.py:18
  91.0 39.6 %collective-permute-start.3 = (bf16[1,4,32,384]{3,2,1,0:T(8,128)(2,1)S(1)}, bf16[1,4,32,384]{3,2,1,0:T(8,128)(2,1)S(1)}, u32[]{:S(2)}, u32[]{:S(2)}) collective-permute-start(bf16[1,4,32,384]{3,2,1,0:T(8,128)(2,1)S(1)} %pad_maximum_fusion.3), channel_id=1, source_target_pairs={{28,0},{0,4},{4,8},{8,12},{12,16},{16,20},{20,24},{24,28},{29,1},{... | collective-permute-start | bytes 294920 | tf_op jit(solution)/shard_map/ppermute | solution.py:18
Sparse Core Ops, SparseCore 0:
  73.0 11.1 reduce-scatter.4
  87.0 19.1 reduce-scatter.2
where the time goes:
time: 218 us; the launch traced here: 214 us
  blocking collectives  115 us (53%)
  matrix products  32.7 us (15%)
  local copies, waits for them, and re-layouts  22.7 us (10%)
  other arithmetic  16.8 us (8%)
  between operations  14.7 us (7%)
  starting transfers between devices  8.08 us (4%)
  waiting for transfers between devices  4.03 us (2%)
    psum x1, blocking collectives, shards(): half_qkv, half_proj = lax.psum((half_qkv, half_proj), ('ha', 'wa'))  75.2 us
    psum x1, blocking collectives, shards(): lax.psum((d_table, d_scale, d_gain), ('ha', 'wa', 'ba'))  39.5 us
    dot_general x3, matrix products, fine_product(): return jnp.einsum(form, left, right, precision=HIGHEST)  16.3 us
    ppermute x4, starting transfers between devices, from_behind(): return lax.ppermute(block, axis, route)  7.79 us
    convert_element_type x2, local copies, waits for them, and re-layouts, grads_region(): jnp.stack([d_query, d_key, d_values], 3).astype(jnp.bfloat16)  5.15 us
    dot_general x3, matrix products, coarse_product(): return jnp.einsum(form, left, right, preferred_element_type=jnp.float32)  5.11 us
  transfers between devices with their start and end apart: 6, of which 2 were waited for; matrix products, arithmetic and copies ran while one was open for 10% of the time, Pallas kernels for 0%

commit v1 on v0

--- a/solution.py
+++ b/solution.py
@@ -179,7 +179,7 @@
             d_wproj.astype(jnp.bfloat16), "ba", scatter_dimension=1, tiled=True
         ).astype(jnp.float32),
     )
-    half_qkv, half_proj = lax.psum((half_qkv, half_proj), ("ha", "wa"))
+    half_qkv, half_proj = lax.psum(lax.psum((half_qkv, half_proj), "ha"), "wa")
     d_table, d_scale, d_gain = lax.psum((d_table, d_scale, d_gain), ("ha", "wa", "ba"))
     return (d_tokens, half_qkv, half_proj, d_table, d_scale, d_gain)
 

time: 218 us -> 226 us (1.037)
  waiting for transfers between devices: 4.03 us -> 25 us
  blocking collectives: 115 us -> 100 us
    reduce_scatter x1, waiting for transfers between devices: 0.01 us -> 21 us  [shards(): lax.psum_scatter(d_wqkv.astype(jnp.bfloat16), 'ba', scatter_dimension=1,...]
    psum x1, blocking collectives: 75.2 us -> 59.6 us  [shards(): half_qkv, half_proj = lax.psum(lax.psum((half_qkv, half_proj), 'ha'), 'wa')]
    unnamed x38 -> x42, local copies, waits for them, and re-layouts: 3.95 us -> 5.92 us
  transfers between devices with their start and end apart: 6 -> 7, of which waited for: 2 -> 3; matrix products, arithmetic and copies ran while one was open for 10% -> 9% of each run, Pallas kernels for 0% -> 0%
where the time goes in v1:
time: 226 us; the launch traced here: 222 us
  blocking collectives  100 us (44%)
  matrix products  32.7 us (14%)
  waiting for transfers between devices  25 us (11%)
  local copies, waits for them, and re-layouts  24.7 us (11%)
  other arithmetic  16.8 us (7%)
  between operations  14.5 us (6%)
  starting transfers between devices  8.09 us (4%)
    psum x1, blocking collectives, shards(): half_qkv, half_proj = lax.psum(lax.psum((half_qkv, half_proj), 'ha'), 'wa')  59.6 us
    psum x1, blocking collectives, shards(): lax.psum((d_table, d_scale, d_gain), ('ha', 'wa', 'ba'))  40.5 us
    reduce_scatter x1, waiting for transfers between devices, shards(): lax.psum_scatter(d_wqkv.astype(jnp.bfloat16), 'ba', scatter_dimension=1,...  21 us
    dot_general x3, matrix products, fine_product(): return jnp.einsum(form, left, right, precision=HIGHEST)  16.3 us
    ppermute x4, starting transfers between devices, from_behind(): return lax.ppermute(block, axis, route)  7.76 us
    unnamed x42, local copies, waits for them, and re-layouts  5.92 us
    convert_element_type x2, local copies, waits for them, and re-layouts, grads_region(): jnp.stack([d_query, d_key, d_values], 3).astype(jnp.bfloat16)  5.15 us
    dot_general x3, matrix products, coarse_product(): return jnp.einsum(form, left, right, preferred_element_type=jnp.float32)  5.11 us
  transfers between devices with their start and end apart: 7, of which 3 were waited for; matrix products, arithmetic and copies ran while one was open for 9% of the time, Pallas kernels for 0%

profile of v1, /device:TPU:0, one launch (start us, length us, event | category | flops | bytes accessed | tf_op | source)
XLA Modules:
  0.0 221.9 jit_solution(15446519817488703582)
XLA Ops:
  7.2 1.0 pad_maximum_fusion.2
  8.3 4.6 %collective-permute-start = (bf16[2,1,4,32,384]{4,3,2,1,0:T(8,128)(2,1)S(1)}, bf16[2,1,4,32,384]{4,3,2,1,0:T(8,128)(2,1)S(1)}, u32[]{:S(2)}, u32[]{:S(2)}) collective-permute-start(bf16[2,1,4,32,384]{4,3,2,1,0:T(8,128)(2,1)S(1)} %pad_maximum_fusion.2), channel_id=1, source_target_pairs={{4,0},{8,4},{12,8},{16,12},{20,16},{24,20},{28,24},{0,28},{5,1},{9... | collective-permute-start | bytes 589832 | tf_op jit(solution)/shard_map/ppermute | solution.py:18
  12.8 1.1 fusion.52
  14.2 0.8 compare_select_fusion
  15.2 2.0 fusion.2
  17.4 0.9 copy.85
  18.3 1.6 collective-permute-start.1
  20.2 2.8 %collective-permute-done.1 = bf16[2,1,16,4,384]{4,3,2,1,0:T(4,128)(2,1)S(1)} collective-permute-done((bf16[2,1,16,4,384]{4,3,2,1,0:T(4,128)(2,1)S(1)}, bf16[2,1,16,4,384]{4,3,2,1,0:T(4,128)(2,1)S(1)}, u32[]{:S(2)}, u32[]{:S(2)}) %collective-permute-start.1) | collective-permute-done | bytes 98336 | tf_op jit(solution)/shard_map/ppermute | solution.py:18
  23.0 0.9 fusion.57
  24.0 0.7 copy-done.9
  24.7 0.8 convolution_convert_fusion
  25.5 0.6 copy.82
  26.1 3.0 %reshape.449 = bf16[1,8,64,3,12,32]{2,1,5,4,3,0:T(8,128)(2,1)} reshape(bf16[512,1152]{0,1:T(8,128)(2,1)S(1)} %copy.82) | data formatting | bytes 2359296 | tf_op jit(solution)/shard_map/reshape | solution.py:79
  29.2 1.8 fusion.67
  31.7 5.2 %fusion.29 = f32[8,12,64,64]{2,3,1,0:T(8,128)S(1)} fusion(f32[8,64,12]{1,2,0:T(8,128)S(1)} %add_rsqrt_fusion.1, f32[8,64,12]{1,2,0:T(8,128)S(1)} %add_rsqrt_fusion, bf16[1,8,64,1,12,32]{2,1,5,4,3,0:T(8,128)(2,1)S(1)} %get-tuple-element.18, bf16[1,8,64,1,12,32]{2,1,5,4,3,0:T(8,128)(2,1)S(1)} %get-tuple-element.19), kind=kOutput, calls=%fused_computation.41 | convolution fusion | flops 151781376 | bytes 2408448 | tf_op jit(solution)/shard_map/bnqhd,bnkhd->bnhqk/dot_general | solution.py:26
  36.9 1.2 fusion.68
  38.6 0.5 fusion.40
  39.2 1.1 copy-done.3
  40.8 1.3 reshape.451
  42.1 1.6 fusion.69
  43.9 0.9 copy.89
  44.8 2.3 %copy.90 = f32[512,384]{0,1:T(8,128)} copy(f32[512,384]{1,0:T(8,128)} %bitcast.140) | data formatting | bytes 1572864 | tf_op jit(solution)/shard_map/convert_element_type | solution.py:109
  47.1 1.2 fusion.42
  48.3 1.4 multiply_reduce_fusion.2
  49.8 1.4 multiply_convert_fusion
  51.7 1.1 convolution_convert_fusion.5
  53.0 1.3 reshape.452
  54.3 3.6 %multiply_reduce_fusion.1 = (f32[8,12,64]{2,1,0:T(8,128)S(1)}, f32[8,12,64,64]{2,3,1,0:T(8,128)S(1)}) fusion(f32[8,12,64,64]{2,3,1,0:T(8,128)} %copy-done.3, f32[8,12,64]{2,1,0:T(8,128)S(1)} %get-tuple-element.23, bf16[1,8,64,1,12,32]{2,1,5,4,3,0:T(8,128)(2,1)} %copy-done.14, bf16[8,64,12,32]{1,0,3,2:T(8,128)(2,1)} %reshape.452), kind=kOutput, calls=%fused_computation.7 | convolution fusion | flops 26339328 | bytes 3981312 | tf_op jit(solution)/shard_map/bnqhd,bnkhd->bnhqk/dot_general | solution.py:22
  57.9 0.6 copy-done.4
  58.6 2.2 multiply_reduce_fusion
  60.7 4.3 %fusion.22 = (f32[8,64,12]{1,2,0:T(8,128)S(1)}, f32[8,12,32,64]{3,2,1,0:T(8,128)}) fusion(f32[8,64,12]{1,2,0:T(8,128)S(1)} %add_rsqrt_fusion.1, bf16[1,8,64,1,12,32]{2,1,5,4,3,0:T(8,128)(2,1)S(1)} %get-tuple-element.19, f32[8,12,64,64]{2,3,1,0:T(8,128)S(1)} %get-tuple-element.17, f32[12]{0:T(128)S(1)} %minimum_exponential_fusion, ...), kind=kOutput, calls=%fused_computation.35 | convolution fusion | flops 152561664 | bytes 3219504 | tf_op jit(solution)/shard_map/bnhqk,bnkhd->bnqhd/dot_general | solution.py:26
  65.0 6.8 %fusion.18 = (f32[8,64,12]{1,2,0:T(8,128)}, f32[8,12,32,64]{3,2,1,0:T(8,128)}) fusion(f32[8,64,12]{1,2,0:T(8,128)S(1)} %add_rsqrt_fusion, bf16[1,8,64,1,12,32]{2,1,5,4,3,0:T(8,128)(2,1)S(1)} %get-tuple-element.18, f32[8,12,64,64]{2,3,1,0:T(8,128)S(1)} %get-tuple-element.17, f32[12]{0:T(128)S(1)} %minimum_exponential_fusion, ...), kind=kOutput, calls=%fused_computation.31 | convolution fusion | flops 152561664 | bytes 3219504 | tf_op jit(solution)/shard_map/bnhqk,bnqhd->bnkhd/dot_general | solution.py:26
  71.9 0.9 convolution_bitcast_fusion
  73.1 2.6 %fusion.21 = (bf16[1,8,64,1,12,32]{2,5,4,1,3,0:T(8,128)(2,1)S(1)}, bf16[1,8,64,1,12,32]{2,5,4,1,3,0:T(8,128)(2,1)S(1)}) fusion(f32[8,12,32,64]{3,2,1,0:T(8,128)} %get-tuple-element.30, f32[8,64,12]{1,2,0:T(8,128)} %get-tuple-element.29, f32[8,64,12]{1,2,0:T(8,128)S(1)} %add_rsqrt_fusion, bf16[1,8,64,1,12,32]{2,1,5,4,3,0:T(8,128)(2,1)S(1)} %get-tuple-element.18, ...), kind=kLoop, calls=%fused_computation.34 | loop fusion | flops 2359296 | bytes 3244032 | tf_op jit(solution)/shard_map/stack | solution.py:135
  75.7 0.6 maximum_convert_fusion
  76.3 2.7 %copy.98 = bf16[1,8,64,3,12,32]{2,1,5,4,3,0:T(8,128)(2,1)S(1)} copy(bf16[1,8,64,3,12,32]{2,5,4,1,3,0:T(8,128)(2,1)S(1)} %maximum_convert_fusion) | data formatting | bytes 2359296 | tf_op jit(solution)/shard_map/convert_element_type | solution.py:135
  79.1 2.4 %convert_element_type.207 = bf16[512,1152]{0,1:T(8,128)(2,1)} reshape(bf16[1,8,64,3,12,32]{2,1,5,4,3,0:T(8,128)(2,1)S(1)} %copy.98) | data formatting | bytes 2359296 | tf_op jit(solution)/shard_map/convert_element_type | solution.py:135
  81.5 3.1 %convolution_convert_fusion.1 = bf16[384,1152]{0,1:T(8,128)(2,1)} fusion(bf16[512,1152]{0,1:T(8,128)(2,1)} %convert_element_type.207, bf16[512,384]{1,0:T(8,128)(2,1)} %bitcast.142), kind=kOutput, calls=%fused_computation.15 | convolution fusion | flops 453427200 | bytes 2457600 | tf_op jit(solution)/shard_map/dot_general | solution.py:136
  84.6 21.0 %reduce-scatter.3.cloned.1.call-done = bf16[384,576]{0,1:T(8,128)(2,1)} async-done(((bf16[384,1152]{0,1:T(8,128)(2,1)}), bf16[384,576]{0,1:T(8,128)(2,1)}) %reduce-scatter.3.cloned.1.call-update) | async-done | bytes 442384 | tf_op jit(solution)/shard_map/reduce_scatter | solution.py:175
  105.6 59.6 %all-reduce.7 = (f32[384,576]{0,1:T(8,128)}, f32[384,192]{0,1:T(8,128)}) all-reduce(bf16[384,576]{0,1:T(8,128)(2,1)} %reduce-scatter.3.cloned.1.call-done, bf16[384,192]{0,1:T(8,128)(2,1)} %reduce-scatter.5.cloned.1.call-done), channel_id=1, replica_groups=mesh['ha'=8,'wa'=2,'ba'=2] {'ha'}, use_global_device_ids=true, to_apply=%region_12.13 | all-reduce | flops 294912 | bytes 1769472 | tf_op jit(solution)/shard_map/psum | solution.py:182
  165.5 0.9 convolution_convert_fusion.3
  166.5 1.5 collective-permute-start.2
  168.0 1.4 fusion.41
  169.5 1.2 collective-permute-done.2
  170.8 40.5 %all-reduce = (f32[12,225]{1,0:T(8,128)}, f32[12]{0:T(128)}, f32[384]{0:T(512)}) all-reduce(f32[12,225]{1,0:T(8,128)S(1)} %fusion.41, f32[12]{0:T(128)S(1)} %compare_select_fusion.1, f32[384]{0:T(512)S(1)} %get-tuple-element.8), channel_id=1, replica_groups=mesh['ha'=8,'wa'=2,'ba'=2] {'ha','wa','ba'}, use_global_device_ids=true, to_apply=%region_18.19 | all-reduce | flops 3096 | bytes 24768 | tf_op jit(solution)/shard_map/psum | solution.py:183
  211.3 0.9 add_convert_fusion
  212.2 2.2 copy.152
  214.4 0.7 copy.153
  (82 shorter events, 4.4 us)
Async XLA Ops:
  7.2 17.5 %copy-start = (bf16[384,1152]{1,0:T(8,128)(2,1)S(1)}, bf16[384,1152]{1,0:T(8,128)(2,1)}, u32[]{:S(2)}) copy-start(bf16[384,1152]{1,0:T(8,128)(2,1)} %param.9) | copy-start | bytes 2654212
  7.2 8.0 %copy-start.18 = (f32[12,225]{1,0:T(8,128)S(1)}, f32[12,225]{1,0:T(8,128)}, u32[]{:S(2)}) copy-start(f32[12,225]{1,0:T(8,128)} %param.11) | copy-start | bytes 32404
  7.2 77.4 %reduce-scatter.5.cloned.1.call-start = ((), (), s32[]{:S(2)}) async-start(), calls=%async_computation.3 | async-start | bytes 442368 | tf_op jit(solution)/shard_map/reduce_scatter | solution.py:178
  8.3 10.0 %collective-permute-start = (bf16[2,1,4,32,384]{4,3,2,1,0:T(8,128)(2,1)S(1)}, bf16[2,1,4,32,384]{4,3,2,1,0:T(8,128)(2,1)S(1)}, u32[]{:S(2)}, u32[]{:S(2)}) collective-permute-start(bf16[2,1,4,32,384]{4,3,2,1,0:T(8,128)(2,1)S(1)} %pad_maximum_fusion.2), channel_id=1, source_target_pairs={{4,0},{8,4},{12,8},{16,12},{20,16},{24,20},{28,24},{0,28},{5,1},{9... | collective-permute-start | bytes 589832 | tf_op jit(solution)/shard_map/ppermute | solution.py:18
  14.0 4.3 %copy-start.19 = (f32[12]{0:T(128)S(1)}, f32[12]{0:T(128)}, u32[]{:S(2)}) copy-start(f32[12]{0:T(128)} %param.12) | copy-start | bytes 148
  18.3 4.7 %collective-permute-start.1 = (bf16[2,1,16,4,384]{4,3,2,1,0:T(4,128)(2,1)S(1)}, bf16[2,1,16,4,384]{4,3,2,1,0:T(4,128)(2,1)S(1)}, u32[]{:S(2)}, u32[]{:S(2)}) collective-permute-start(bf16[2,1,16,4,384]{4,3,2,1,0:T(4,128)(2,1)S(1)} %pad_maximum_fusion.4), channel_id=1, source_target_pairs={{2,0},{0,2},{3,1},{1,3},{6,4},{4,6},{7,5},{5,7},{10,8},{8,10},{11,... | collective-permute-start | bytes 294920 | tf_op jit(solution)/shard_map/ppermute | solution.py:18
  24.0 0.7 copy-start.9
  30.9 7.7 %copy-start.14 = (bf16[1,8,64,1,12,32]{2,1,5,4,3,0:T(8,128)(2,1)}, bf16[1,8,64,1,12,32]{2,1,5,4,3,0:T(8,128)(2,1)S(1)}, u32[]{:S(2)}) copy-start(bf16[1,8,64,1,12,32]{2,1,5,4,3,0:T(8,128)(2,1)S(1)} %get-tuple-element.20) | copy-start | bytes 1179652
  31.7 5.2 %copy-start.10 = (f32[12,64,64]{1,2,0:T(8,128)S(1)}, f32[12,64,64]{1,2,0:T(8,128)}, u32[]{:S(2)}) copy-start(f32[12,64,64]{1,2,0:T(8,128)} %copy.85) | copy-start | bytes 589828
  31.7 5.2 %copy-start.13 = (f32[8,64,64]{1,2,0:T(8,128)S(1)}, f32[8,64,64]{1,2,0:T(8,128)}, u32[]{:S(2)}) copy-start(f32[8,64,64]{1,2,0:T(8,128)} %compare_select_fusion) | copy-start | bytes 393220
  36.9 1.7 copy-start.1
  38.6 1.7 copy-start.3
  42.1 1.7 copy-start.6
  43.9 3.2 %copy-start.17 = (f32[384]{0:T(512)S(1)}, f32[384]{0:T(512)}, u32[]{:S(2)}) copy-start(f32[384]{0:T(512)} %param.13) | copy-start | bytes 4612
  49.8 1.4 copy-start.12
  49.8 1.9 copy-start.5
  54.3 3.6 %copy-start.2 = (f32[8,12,64,64]{2,3,1,0:T(8,128)S(1)}, f32[8,12,64,64]{2,3,1,0:T(8,128)}, u32[]{:S(2)}) copy-start(f32[8,12,64,64]{2,3,1,0:T(8,128)} %copy-done.1) | copy-start | bytes 4718596
  54.3 4.3 %copy-start.4 = (f32[8,12,64,64]{2,3,1,0:T(8,128)S(1)}, f32[8,12,64,64]{2,3,1,0:T(8,128)}, u32[]{:S(2)}) copy-start(f32[8,12,64,64]{2,3,1,0:T(8,128)} %copy-done.3) | copy-start | bytes 4718596
  65.0 6.8 %copy-start.15 = (bf16[8,64,12,32]{1,0,3,2:T(8,128)(2,1)S(1)}, bf16[8,64,12,32]{1,0,3,2:T(8,128)(2,1)}, u32[]{:S(2)}) copy-start(bf16[8,64,12,32]{1,0,3,2:T(8,128)(2,1)} %reshape.452) | copy-start | bytes 1179652
  72.8 32.7 %reduce-scatter.3.cloned.1.call-start = ((), (), s32[]{:S(2)}) async-start(), calls=%async_computation.2 | async-start | bytes 1327104 | tf_op jit(solution)/shard_map/reduce_scatter | solution.py:175
  84.5 80.7 %copy-start.8 = (f32[12,64,64]{1,2,0:T(8,128)S(1)}, f32[12,64,64]{1,2,0:T(8,128)}, u32[]{:S(2)}) copy-start(f32[12,64,64]{1,2,0:T(8,128)} %get-tuple-element.7) | copy-start | bytes 589828
  84.5 81.0 %copy-start.11 = (bf16[512,1152]{0,1:T(8,128)(2,1)S(1)}, bf16[512,1152]{0,1:T(8,128)(2,1)}, u32[]{:S(2)}) copy-start(bf16[512,1152]{0,1:T(8,128)(2,1)} %convert_element_type.207) | copy-start | bytes 3538948
  84.6 127.6 %all-reduce.6.cloned.1.call-start = ((), (), s32[]{:S(2)}) async-start(), calls=%async_computation.4 | async-start | bytes 2359296 | tf_op jit(solution)/shard_map/psum | solution.py:182
  166.4 44.9 %copy-start.7 = (bf16[1,16,32,384]{3,2,1,0:T(8,128)(2,1)S(1)}, bf16[1,16,32,384]{3,2,1,0:T(8,128)(2,1)}, u32[]{:S(2)}) copy-start(bf16[1,16,32,384]{3,2,1,0:T(8,128)(2,1)} %param.8) | copy-start | bytes 1179652
  166.5 4.2 %collective-permute-start.2 = (bf16[1,16,4,384]{3,2,1,0:T(4,128)(2,1)S(1)}, bf16[1,16,4,384]{3,2,1,0:T(4,128)(2,1)S(1)}, u32[]{:S(2)}, u32[]{:S(2)}) collective-permute-start(bf16[1,16,4,384]{3,2,1,0:T(4,128)(2,1)S(1)} %slice.61), channel_id=1, source_target_pairs={{2,0},{0,2},{3,1},{1,3},{6,4},{4,6},{7,5},{5,7},{10,8},{8,10},{11,... | collective-permute-start | bytes 147464 | tf_op jit(solution)/shard_map/ppermute | solution.py:18
  170.7 40.6 %collective-permute-start.3 = (bf16[1,4,32,384]{3,2,1,0:T(8,128)(2,1)S(1)}, bf16[1,4,32,384]{3,2,1,0:T(8,128)(2,1)S(1)}, u32[]{:S(2)}, u32[]{:S(2)}) collective-permute-start(bf16[1,4,32,384]{3,2,1,0:T(8,128)(2,1)S(1)} %pad_maximum_fusion.3), channel_id=1, source_target_pairs={{28,0},{0,4},{4,8},{8,12},{12,16},{16,20},{20,24},{24,28},{29,1},{... | collective-permute-start | bytes 294920 | tf_op jit(solution)/shard_map/ppermute | solution.py:18
  212.2 2.2 copy-start.16
Sparse Core Ops, SparseCore 0:
  73.0 11.1 reduce-scatter.4
  87.0 18.5 reduce-scatter.2
  165.3 41.9 all-reduce.5
